TPU v7x, 32 devices: a whole 2x2x4 slice. The times are simulated.
32 devices in a mesh: dp: 4 (over y, x), owner: 8 (over z, core).
Axes of the slice: x: 2, y: 2, z: 4, core: 2. Of those that a mesh axis runs over, the one named last changes fastest.
Arguments:
- partial_grads: bfloat16 [4, 48, 1024, 1024], P('dp', None, 'owner'), may hold values from -2.09375 to 2.09375
- owner_map: int32 [48], replicated, may hold values from 0 to 7, as said below
- left_stats: float32 [8, 12, 1024, 1024], P('owner', None, 'dp'), may hold values from -1.8 to 1.8
- right_stats: float32 [8, 12, 1024, 1024], P('owner', None, 'dp'), may hold values from -1.8 to 1.8
- left_roots: bfloat16 [8, 12, 1024, 1024], P('owner', None, 'dp'), as said below
- right_roots: bfloat16 [8, 12, 1024, 1024], P('owner', None, 'dp'), as said below
Outputs:
- direction: bfloat16 [48, 1024, 1024], P(None, ('dp', 'owner'))
- new_left_stats: float32 [8, 12, 1024, 1024], P('owner', None, 'dp')
- new_right_stats: float32 [8, 12, 1024, 1024], P('owner', None, 'dp')
Inputs may be any that keep to these rules, and one draw needn't show every extreme that they name: `owner_map`: no owner index holds more than 12 blocks, and some owner holds exactly 12. `left_roots`: each block is dense and not symmetric; its diagonal entries are of order one and its off-diagonal entries are small. `right_roots`: each block is dense and not symmetric; its diagonal entries are of order one and its off-diagonal entries are small.
All inputs are finite; a program needn't handle non-finite values.
Results may differ from a plain program's by a relative error of at most 0.017.
Values may be sent and summed in bfloat16 or wider, within the bound.
A program may use at most 256 MiB of HBM per device.

v0:
```python
import functools

import jax
import jax.numpy as jnp
from jax import lax
from jax.experimental import pallas as pl
from jax.experimental.pallas import tpu as pltpu
from jax.sharding import PartitionSpec as P


D_MODEL = 2560
D_IN = 10576
D_INNER = 5120
TILE = 1024

stat_decay = 0.999


def extents(count):
    index = jnp.arange(count, dtype=jnp.int32)
    in_cols = -(-D_IN // TILE)
    out_cols = -(-D_MODEL // TILE)
    in_count = -(-D_MODEL // TILE) * in_cols
    is_in = index < in_count
    other = jnp.maximum(index - in_count, 0)
    rows = jnp.where(
        is_in,
        jnp.minimum(TILE, D_MODEL - index // in_cols * TILE),
        jnp.minimum(TILE, D_INNER - other // out_cols * TILE),
    )
    cols = jnp.where(
        is_in,
        jnp.minimum(TILE, D_IN - index % in_cols * TILE),
        jnp.minimum(TILE, D_MODEL - other % out_cols * TILE),
    )
    return (rows, cols)


def dot(a, b, dims):
    return lax.dot_general(a, b, (dims, ((), ())), preferred_element_type=jnp.float32)


def step_kernel(base, info, grads, roots, left_roots, left_stats, right_stats, *rest):
    direction, new_left, new_right, left_part = rest[-4:]
    dp, _, _, piece, width = grads.shape
    lanes, tile = left_stats.shape[1:]
    here = info[0]
    pieces = lanes // piece
    full = [grads[d].reshape(tile, width) for d in range(dp)]
    mine = grads[here].reshape(tile, width).T
    gram = None
    for d in range(dp):
        right = dot(mine, full[d], ((1,), (0,)))
        cut = (0, slice(None), slice(d * width, (d + 1) * width))
        new_right[cut] = stat_decay * right_stats[cut] + (1.0 - stat_decay) * right
        part = dot(left_roots[0], full[d], ((1,), (0,)))
        left_part[:, d * width : (d + 1) * width] = part.astype(jnp.bfloat16)
        rows = grads[d, pl.ds(here * pieces, pieces)].reshape(lanes, width)
        term = dot(rows, full[d], ((1,), (1,)))
        gram = term if gram is None else gram + term
    new_left[0] = stat_decay * left_stats[0] + (1.0 - stat_decay) * gram
    product = dot(left_part[...], roots[...].reshape(tile, tile), ((1,), (0,)))
    slot = base + pl.program_id(0)
    row = lax.broadcasted_iota(jnp.int32, product.shape, 0)
    col = lax.broadcasted_iota(jnp.int32, product.shape, 1)
    keep = (row < info[1 + 2 * slot]) & (col < info[2 + 2 * slot])
    result = jnp.where(keep, product, 0.0).astype(jnp.bfloat16)
    direction[...] = result.reshape(direction.shape)


def step(base, chunk, info, grads, roots, left_roots, left_stats, right_stats, carried):
    dp, owners, _, piece, width = grads.shape
    _, lanes, tile = left_stats.shape
    at = lambda s, info: (base + s, 0, 0)
    stats = pl.BlockSpec((1, lanes, tile), at)
    in_specs = [
        pl.BlockSpec((dp, owners, 1, piece, width), lambda s, info: (0, 0, s, 0, 0)),
        pl.BlockSpec((dp, 1, lanes, tile), lambda s, info: (0, base + s, 0, 0)),
        stats,
        stats,
        stats,
    ] + [pl.BlockSpec(memory_space=pl.ANY)] * len(carried)
    sub = lanes // owners
    return pl.pallas_call(
        functools.partial(step_kernel, base),
        grid_spec=pltpu.PrefetchScalarGridSpec(
            num_scalar_prefetch=1,
            grid=(chunk,),
            in_specs=in_specs,
            out_specs=[
                pl.BlockSpec((owners, 1, sub, tile), lambda s, info: (0, s, 0, 0)),
                stats,
                stats,
            ],
            scratch_shapes=[pltpu.VMEM((lanes, tile), jnp.bfloat16)],
        ),
        out_shape=[
            jax.ShapeDtypeStruct((owners, chunk, sub, tile), jnp.bfloat16),
            jax.ShapeDtypeStruct(left_stats.shape, jnp.float32),
            jax.ShapeDtypeStruct(right_stats.shape, jnp.float32),
        ],
        input_output_aliases={6: 1, 7: 2} if carried else {},
        compiler_params=pltpu.CompilerParams(vmem_limit_bytes=48 * 1024 * 1024),
        cost_estimate=pl.CostEstimate(
            flops=8 * chunk * lanes * tile * tile,
            bytes_accessed=chunk * (4 * tile * tile + 20 * lanes * tile),
            transcendentals=0,
        ),
    )(info, grads, roots, left_roots, left_stats, right_stats, *carried)


def chunks_of(slots):
    if slots < 6:
        sizes = (slots,)
    else:
        last, middle = slots // 4, slots // 3
        sizes = (slots - middle - last, middle, last)
    return [(sum(sizes[:index]), size) for index, size in enumerate(sizes)]


def general(partial_grads, owner_map, left_stats, right_stats, left_roots, right_roots):
    dp = lax.axis_size("dp")
    owners = lax.axis_size("owner")
    owner_here = lax.axis_index("owner")
    dp_here = lax.axis_index("dp")
    tiles = owner_map.shape[0]
    slots = left_stats.shape[1]
    lanes = left_stats.shape[2]
    tile = left_stats.shape[3]
    piece = partial_grads.shape[2]
    width = tile // dp
    rows, cols = extents(tiles)
    ids = jnp.arange(tiles, dtype=jnp.int32)
    same = (owner_map[:, None] == owner_map[None, :]) & (ids[None, :] < ids[:, None])
    slot = jnp.sum(same.astype(jnp.int32), axis=1)
    picks = (slot[None, None, :] == jnp.arange(slots, dtype=jnp.int32)[None, :, None]) & (
        owner_map[None, None, :] == jnp.arange(owners, dtype=jnp.int32)[:, None, None]
    )
    tile_of = jnp.sum(jnp.where(picks, ids[None, None, :], 0), axis=2)
    filled = jnp.any(picks, axis=2)

    shares = lax.psum_scatter(partial_grads[0], "dp", scatter_dimension=2, tiled=True)
    roots = lax.all_gather(right_roots[0], "dp", axis=0)

    piece_rows = owner_here * piece + jnp.arange(piece, dtype=jnp.int32)
    piece_cols = dp_here * width + jnp.arange(width, dtype=jnp.int32)
    tile_here = lax.dynamic_index_in_dim(tile_of, owner_here, 0, keepdims=False)
    info = jnp.stack([jnp.take(rows, tile_here) - dp_here * lanes, jnp.take(cols, tile_here)], 1)
    info = jnp.concatenate([dp_here[None], info.reshape(-1)]).astype(jnp.int32)

    spans = chunks_of(slots)
    arrived = []
    for base, chunk in spans:
        which = tile_of[:, base : base + chunk]
        rows_of = jnp.where(filled[:, base : base + chunk], jnp.take(rows, which), 0)
        mask = (piece_rows[:, None] < rows_of[:, :, None, None]) & (
            piece_cols[None, :] < jnp.take(cols, which)[:, :, None, None]
        )
        taken = jnp.take(shares, which.reshape(-1), axis=0).reshape(owners, chunk, piece, width)
        sent = lax.all_to_all(
            jnp.where(mask, taken, jnp.zeros((), shares.dtype)),
            "owner",
            split_axis=0,
            concat_axis=0,
            tiled=True,
        )
        arrived.append(sent)

    def place(index, returned, direction):
        base, chunk = spans[index]
        flat = returned.reshape(owners * chunk, lanes // owners, tile)
        inside = (slot >= base) & (slot < base + chunk)
        at = jnp.where(inside, owner_map * chunk + slot - base, 0)
        return jnp.where(inside[:, None, None], jnp.take(flat, at, axis=0), direction)

    direction = jnp.zeros((tiles, lanes // owners, tile), jnp.bfloat16)
    carried = ()
    for index, (base, chunk) in enumerate(spans):
        grads = lax.all_gather(arrived[index], "dp", axis=0)
        if index:
            direction = place(index - 1, returned, direction)
            grads, direction = lax.optimization_barrier((grads, direction))
        result, *carried = step(
            base, chunk, info, grads, roots, left_roots[0], left_stats[0], right_stats[0], carried
        )
        returned = lax.all_to_all(result, "owner", split_axis=0, concat_axis=0, tiled=True)
    direction = place(len(spans) - 1, returned, direction)
    new_left, new_right = carried
    return (direction, new_left[None], new_right[None])


MESH = pl.DeviceIdType.MESH


def owner_slots(owner_map, owners, slots):
    tiles = owner_map.shape[0]
    ids = jnp.arange(tiles, dtype=jnp.int32)
    same = (owner_map[:, None] == owner_map[None, :]) & (ids[None, :] < ids[:, None])
    slot = jnp.sum(same.astype(jnp.int32), axis=1)
    picks = (slot[None, None, :] == jnp.arange(slots, dtype=jnp.int32)[None, :, None]) & (
        owner_map[None, None, :] == jnp.arange(owners, dtype=jnp.int32)[:, None, None]
    )
    tile_of = jnp.sum(jnp.where(picks, ids[None, None, :], 0), axis=2)
    return slot, tile_of, jnp.any(picks, axis=2)


def exchange_kernel(
    counts, sent, roots, left_roots, left_stats, right_stats,
    returned, new_left, new_right, wide,
    g_v, r_v, l_v, ls_v, rs_v, part_v, mine_v, out_v, nl_v, nr_v,
    own_sem, to_send, to_recv, wide_send, wide_recv, back_send, back_recv, back_own,
    g_sem, r_sem, in_sem, nl_sem, nr_sem,
):
    owners, slots, strip, tile = sent.shape
    lanes = left_roots.shape[1]
    parities = len(counts)
    panels = wide.shape[1]
    half = owners // 2
    pieces = lanes // (tile // owners)
    own = lax.axis_index("owner")
    me = lax.axis_index("dp")
    across = me + 1 - 2 * (me % 2)
    along = me + 2 - 4 * (me // 2)
    far = 3 - me
    kind = own % parities
    many = sum(jnp.where(kind == p, counts[p], 0) for p in range(parities))
    others = [(own + j) % owners for j in range(1, owners)]

    barrier = pltpu.get_barrier_semaphore()
    for peer in (across, along):
        pl.semaphore_signal(barrier, inc=1, device_id={"dp": peer}, device_id_type=MESH)
    for peer in others:
        pl.semaphore_signal(barrier, inc=1, device_id={"owner": peer}, device_id_type=MESH)
    pl.semaphore_wait(barrier, owners + 1)

    def each(low, high, act):
        lax.fori_loop(low, high, lambda i, c: (act(i), c)[1], 0)

    def place_of(item):
        return jnp.where(item < many, item, slots + item - many)

    def own_copy(s):
        return pltpu.make_async_copy(
            sent.at[own, s], wide.at[slots + s, me, own], own_sem.at[s]
        )

    def give(s, peer):
        return pltpu.make_async_remote_copy(
            src_ref=sent.at[peer, s],
            dst_ref=wide.at[slots + s, me, own],
            send_sem=to_send.at[peer % parities, s],
            recv_sem=to_recv.at[s],
            device_id={"owner": peer},
            device_id_type=MESH,
        )

    def direct(src, place, axis, peer):
        return pltpu.make_async_remote_copy(
            src_ref=src,
            dst_ref=wide.at[place, me],
            send_sem=wide_send.at[place, axis],
            recv_sem=wide_recv.at[place, axis],
            device_id={"dp": peer},
            device_id_type=MESH,
        )

    def forward(place, axis, panel, first, peer):
        piece = wide.at[place, panel, pl.ds(first, half)]
        return pltpu.make_async_remote_copy(
            src_ref=piece,
            dst_ref=piece,
            send_sem=wide_send.at[place, axis],
            recv_sem=wide_recv.at[place, axis],
            device_id={"dp": peer},
            device_id_type=MESH,
        )

    def sized(ref, sem):
        return pltpu.make_async_copy(ref, ref, sem)

    def loads(s):
        made = [pltpu.make_async_copy(roots.at[s], r_v.at[me], r_sem.at[0])]
        for index, panel in enumerate((across, along, far)):
            made.append(
                pltpu.make_async_copy(wide.at[s, panel], r_v.at[panel], r_sem.at[1 + index])
            )
        made.append(pltpu.make_async_copy(left_roots.at[s], l_v, in_sem.at[0]))
        made.append(pltpu.make_async_copy(left_stats.at[s], ls_v, in_sem.at[1]))
        made.append(pltpu.make_async_copy(right_stats.at[s], rs_v, in_sem.at[2]))
        return made

    def grads(s):
        return [
            pltpu.make_async_copy(wide.at[slots + s, j], g_v.at[:, j], g_sem.at[j])
            for j in range(panels)
        ]

    def back(s, side, peer):
        return pltpu.make_async_remote_copy(
            src_ref=out_v.at[side, peer],
            dst_ref=returned.at[own, s],
            send_sem=back_send.at[side],
            recv_sem=back_recv.at[kind, s],
            device_id={"owner": peer},
            device_id_type=MESH,
        )

    def back_home(s, side):
        return pltpu.make_async_copy(out_v.at[side, own], returned.at[own, s], back_own.at[side])

    def stats_out(s, side):
        return (
            pltpu.make_async_copy(nl_v.at[side], new_left.at[s], nl_sem.at[side]),
            pltpu.make_async_copy(nr_v.at[side], new_right.at[s], nr_sem.at[side]),
        )

    def settle(s, side):
        sized(returned.at[0, pl.ds(0, owners - 1)], back_send.at[side]).wait()
        back_home(s, side).wait()
        for copy in stats_out(s, side):
            copy.wait()

    width = lanes

    def compute(s):
        side = s % 2
        for copy in grads(s):
            copy.start()

        @pl.when(s == 0)
        def _():
            for copy in loads(0):
                copy.start()

        @pl.when(s >= 2)
        def _():
            settle(s - 2, side)

        for copy in grads(s) + loads(s):
            copy.wait()

        def cols(c):
            return pl.ds(pl.multiple_of(c * width, width), width)

        def column(c):
            return g_v[:, :, :, cols(c)].reshape(tile, width)

        def first(c):
            part = dot(l_v[...], column(c), ((1,), (0,)))
            part_v[:, cols(c)] = part.astype(jnp.bfloat16)

        def second(c):
            right = r_v[:, :, :, cols(c)].reshape(tile, width)
            product = dot(part_v[...], right, ((1,), (0,)))
            out_v[side, :, :, cols(c)] = product.astype(jnp.bfloat16).reshape(owners, strip, width)

        each(0, tile // width, first)
        each(0, tile // width, second)
        for peer in others:
            back(s, side, peer).start()
        back_home(s, side).start()
        mine_v[...] = column(me).T

        def third(c):
            right = dot(mine_v[...], column(c), ((1,), (0,)))
            nr_v[side, :, cols(c)] = stat_decay * rs_v[:, cols(c)] + (1.0 - stat_decay) * right
            rows = g_v[pl.ds(me * pieces, pieces)].reshape(lanes, tile)
            block = g_v[pl.ds(c * pieces, pieces)].reshape(lanes, tile)
            left = dot(rows, block, ((1,), (1,)))
            nl_v[side, :, cols(c)] = stat_decay * ls_v[:, cols(c)] + (1.0 - stat_decay) * left

        each(0, tile // width, third)
        for copy in stats_out(s, side):
            copy.start()

        @pl.when(s + 1 < many)
        def _():
            for copy in loads(s + 1):
                copy.start()

    each(0, many, lambda s: own_copy(s).start())

    def turn(i):
        @pl.when(i < many)
        def _():
            direct(roots.at[i], i, 0, across).start()
            direct(roots.at[i], i, 1, along).start()

        @pl.when(i < slots)
        def _():
            for peer in others:
                if min(counts) == slots:
                    give(i, peer).start()
                else:
                    for p in range(parities):
                        @pl.when((peer % parities == p) & (i < counts[p]))
                        def _():
                            give(i, peer).start()

        @pl.when((i >= many) & (i < 2 * many))
        def _():
            s = i - many
            own_copy(s).wait()
            sized(wide.at[slots + s, me, pl.ds(0, owners - 1)], to_recv.at[s]).wait()
            direct(wide.at[slots + s, me], slots + s, 0, across).start()
            direct(wide.at[slots + s, me], slots + s, 1, along).start()

        @pl.when((i >= 1) & (i < 2 * many + 1))
        def _():
            place = place_of(i - 1)
            sized(wide.at[place, across], wide_recv.at[place, 0]).wait()
            forward(place, 2, across, 0, along).start()
            sized(wide.at[place, along], wide_recv.at[place, 1]).wait()
            forward(place, 3, along, half, across).start()

        @pl.when(i >= 2)
        def _():
            place = place_of(i - 2)
            sized(wide.at[place, far, pl.ds(0, half)], wide_recv.at[place, 2]).wait()
            sized(wide.at[place, far, pl.ds(half, half)], wide_recv.at[place, 3]).wait()

        @pl.when(i >= many + 2)
        def _():
            compute(i - 2 - many)

    each(0, 2 * many + 2, turn)

    settle(many - 2, many % 2)
    settle(many - 1, (many + 1) % 2)

    if min(counts) < slots:
        def fade(s):
            moved = [
                pltpu.make_async_copy(left_stats.at[s], ls_v, in_sem.at[1]),
                pltpu.make_async_copy(right_stats.at[s], rs_v, in_sem.at[2]),
            ]
            for copy in moved:
                copy.start()
            for copy in moved:
                copy.wait()
            nl_v[0] = stat_decay * ls_v[...]
            nr_v[0] = stat_decay * rs_v[...]
            for copy in stats_out(s, 0):
                copy.start()
            for copy in stats_out(s, 0):
                copy.wait()

        each(many, slots, fade)

    def sends(item):
        place = place_of(item)
        panel = wide.at[place, me]
        part = wide.at[place, me, pl.ds(0, half)]
        sized(panel, wide_send.at[place, 0]).wait()
        sized(panel, wide_send.at[place, 1]).wait()
        sized(part, wide_send.at[place, 2]).wait()
        sized(part, wide_send.at[place, 3]).wait()

    each(0, 2 * many, sends)
    group = owners // parities
    for p in range(parities):
        def ends(s, p=p):
            for alike in (True, False):
                size = group - 1 if alike else group

                @pl.when((kind == p) == alike)
                def _():
                    piece = sent.at[0, pl.ds(0, size)]
                    sized(piece, to_send.at[p, s]).wait()
                    sized(piece, back_recv.at[p, s]).wait()

        each(0, counts[p], ends)


def exchange(counts, sent, roots, left_roots, left_stats, right_stats):
    owners, slots, strip, tile = sent.shape
    lanes = left_stats.shape[1]
    dp = tile // lanes
    anywhere = pl.BlockSpec(memory_space=pl.ANY)
    bf16, f32 = jnp.bfloat16, jnp.float32
    dma = pltpu.SemaphoreType.DMA
    return pl.pallas_call(
        functools.partial(exchange_kernel, counts),
        in_specs=[pl.BlockSpec(memory_space=pltpu.VMEM)] + [anywhere] * 4,
        out_specs=[anywhere] * 4,
        out_shape=[
            jax.ShapeDtypeStruct((owners, slots, strip, tile), bf16),
            jax.ShapeDtypeStruct(left_stats.shape, f32),
            jax.ShapeDtypeStruct(right_stats.shape, f32),
            jax.ShapeDtypeStruct((2 * slots, dp, owners, strip, tile), bf16),
        ],
        scratch_shapes=[
            pltpu.VMEM((owners, dp, strip, tile), bf16),
            pltpu.VMEM((dp, owners, strip, tile), bf16),
            pltpu.VMEM((lanes, tile), bf16),
            pltpu.VMEM((lanes, tile), f32),
            pltpu.VMEM((lanes, tile), f32),
            pltpu.VMEM((lanes, tile), bf16),
            pltpu.VMEM((lanes, tile), bf16),
            pltpu.VMEM((2, owners, strip, tile), bf16),
            pltpu.VMEM((2, lanes, tile), f32),
            pltpu.VMEM((2, lanes, tile), f32),
            dma((slots,)),
            dma((len(counts), slots)),
            dma((slots,)),
            dma((2 * slots, 4)),
            dma((2 * slots, 4)),
            dma((2,)),
            dma((len(counts), slots)),
            dma((2,)),
            dma((dp,)),
            dma((dp,)),
            dma((3,)),
            dma((2,)),
            dma((2,)),
        ],
        compiler_params=pltpu.CompilerParams(
            collective_id=0, has_side_effects=True, vmem_limit_bytes=40 * 1024 * 1024
        ),
        cost_estimate=pl.CostEstimate(
            flops=8 * slots * lanes * tile * tile,
            bytes_accessed=slots * (12 * tile * tile + 20 * lanes * tile),
            transcendentals=0,
        ),
        name="exchange",
    )(sent, roots, left_roots, left_stats, right_stats)


def inner(partial_grads, owner_map, left_stats, right_stats, left_roots, right_roots):
    dp = lax.axis_size("dp")
    owners = lax.axis_size("owner")
    slots, lanes, tile = left_stats.shape[1:]
    if dp != 4 or owners % 2 or slots < 2:
        return general(
            partial_grads, owner_map, left_stats, right_stats, left_roots, right_roots
        )
    owner_here = lax.axis_index("owner")
    dp_here = lax.axis_index("dp")
    tiles = owner_map.shape[0]
    strip = lanes // owners
    rows, cols = extents(tiles)
    slot, tile_of, filled = owner_slots(owner_map, owners, slots)
    line = jnp.arange(strip, dtype=jnp.int32)
    wide_line = jnp.arange(tile, dtype=jnp.int32)
    shares = lax.psum_scatter(partial_grads[0], "dp", scatter_dimension=1, tiled=True)
    first = owner_here * (tile // owners) + dp_here * strip
    which = tile_of.reshape(-1)
    rows_of = jnp.where(filled.reshape(-1), jnp.take(rows, which), 0)
    cols_of = jnp.take(cols, which)
    keep = ((first + line)[None, :, None] < rows_of[:, None, None]) & (
        wide_line[None, None, :] < cols_of[:, None, None]
    )
    taken = jnp.take(shares, which, axis=0)
    sent = jnp.where(keep, taken, jnp.zeros((), taken.dtype))
    counts = (slots, slots)
    shape = (slots, owners, strip, tile)
    returned, new_left, new_right, _ = exchange(
        counts,
        sent.reshape(owners, slots, strip, tile),
        right_roots[0].reshape(shape),
        left_roots[0],
        left_stats[0],
        right_stats[0],
    )
    first = dp_here * lanes + owner_here * strip
    inside = ((first + line)[None, :, None] < rows[:, None, None]) & (
        wide_line[None, None, :] < cols[:, None, None]
    )
    flat = returned.reshape(owners * slots, strip, tile)
    direction = jnp.take(flat, owner_map * slots + slot, axis=0)
    direction = jnp.where(inside, direction, jnp.zeros((), direction.dtype))
    return (direction, new_left[None], new_right[None])


def solution(mesh):
    placed = (
        P("dp", None, "owner", None),
        P(),
        P("owner", None, "dp", None),
        P("owner", None, "dp", None),
        P("owner", None, "dp", None),
        P("owner", None, "dp", None),
    )
    return jax.shard_map(
        inner,
        mesh=mesh,
        in_specs=placed,
        out_specs=(
            P(None, ("dp", "owner"), None),
            P("owner", None, "dp", None),
            P("owner", None, "dp", None),
        ),
        check_vma=False,
    )
```

profile of v0, /device:TPU:1, one launch (start us, length us, event | category | flops | bytes accessed | tf_op | source)
XLA Modules:
  0.0 619.2 jit_solution(12620682041712385338)
XLA Ops:
  7.2 0.7 reduce-scatter.2.cloned.1.call-update
  7.9 0.2 convert_reduce_fusion
  8.1 0.3 fusion
  8.4 0.1 copy.10
  8.5 0.1 reshape.285
  8.6 0.1 reshape.286
  8.7 1.2 gather_fusion.2
  9.9 1.2 gather_fusion.3
  11.2 0.3 and_reduce_fusion
  11.5 0.1 copy.9
  11.6 0.1 reshape.284
  11.9 0.1 copy.11
  12.1 0.1 broadcast_compare_fusion
  12.2 0.1 iota_compare_fusion.1
  12.3 0.1 iota_compare_fusion
  12.4 121.2 %reduce-scatter.2.cloned.1.call-done = bf16[48,32,1024]{2,1,0:T(8,128)(2,1)} async-done(((bf16[48,128,1024]{2,1,0:T(8,128)(2,1)}), bf16[48,32,1024]{2,1,0:T(8,128)(2,1)}) %reduce-scatter.2.cloned.1.call-update) | async-done | bytes 3145744 | tf_op jit(solution)/shard_map/reduce_scatter | solution.py:545
  133.6 7.9 %gather_fusion = bf16[96,32,1024]{2,1,0:T(8,128)(2,1)} fusion(bf16[48,32,1024]{2,1,0:T(8,128)(2,1)} %reduce-scatter.2.cloned.1.call-done, s32[1024]{0:T(1024)S(1)} %pad_clamp_fusion.1), kind=kCustom, calls=%fused_computation.2 | custom fusion | bytes 12583296 | tf_op jit(solution)/shard_map/jit(_take)/gather | solution.py:553
  141.5 5.1 and_select_fusion.sent
  146.6 432.6 %exchange.1 = (bf16[8,12,32,1024]{3,2,1,0:T(8,128)(2,1)S(1)}, f32[12,256,1024]{2,1,0:T(8,128)}, f32[12,256,1024]{2,1,0:T(8,128)}, bf16[24,4,8,32,1024]{4,3,2,1,0:T(8,128)(2,1)}) custom-call(bf16[8,12,32,1024]{3,2,1,0:T(8,128)(2,1)S(1)} %and_select_fusion.sent, bf16[12,8,32,1024]{3,2,1,0:T(8,128)(2,1)} %bitcast.18, bf16[12,256,1024]{2,1,0:T(8,128)(2,1)} %bitcast.19, ...), custom_call_target="tpu_custom_call" | custom-call | flops 25769803776 | bytes 213909504 | tf_op jit(solution)/shard_map/exchange/pallas_call | solution.py:482
  579.2 2.7 copy-done
  581.9 3.5 gather_fusion.1
  585.5 2.7 and_select_fusion.1
  588.2 12.1 %copy.15 = f32[1,12,256,1024]{3,2,1,0:T(8,128)} copy(f32[1,12,256,1024]{3,2,1,0:T(8,128)} %bitcast.15) | data formatting | bytes 25165824
  600.3 12.1 %copy.16 = f32[1,12,256,1024]{3,2,1,0:T(8,128)} copy(f32[1,12,256,1024]{3,2,1,0:T(8,128)} %bitcast.14) | data formatting | bytes 25165824
  (21 shorter events, 0.4 us)
Async XLA Ops:
  7.2 126.4 %reduce-scatter.2.cloned.1.call-start = ((), (), s32[]{:S(2)}) async-start(), calls=%async_computation.1 | async-start | bytes 15728640 | tf_op jit(solution)/shard_map/reduce_scatter | solution.py:545
  7.2 0.7 copy-start.1
  579.2 2.7 copy-start
Sparse Core Ops, SparseCore 0:
  11.1 122.4 reduce-scatter.1
where the time goes:
time: 621 us; the launch traced here: 619 us
  Pallas kernels  433 us (70%)
  waiting for transfers between devices  122 us (20%)
  local copies, waits for them, and re-layouts  41.4 us (7%)
  between operations  14.2 us (2%)
  other arithmetic  9.06 us (1%)
    pallas_call x1, Pallas kernels, exchange(): pl.pallas_call(functools.partial(exchange_kernel, counts), in_specs=[pl.B...  433 us
    reduce_scatter x1, waiting for transfers between devices, inner(): lax.psum_scatter(partial_grads[0], 'dp', scatter_dimension=1, tiled=True)  121 us
    unnamed x6, local copies, waits for them, and re-layouts  26.9 us
  transfers between devices with their start and end apart: 1, of which 1 were waited for; matrix products, arithmetic and copies ran while one was open for 1% of the time, Pallas kernels for 0%

commit v1 on v0

--- a/solution.py
+++ b/solution.py
@@ -472,7 +472,7 @@
         each(0, counts[p], ends)
 
 
-def exchange(counts, sent, roots, left_roots, left_stats, right_stats):
+def exchange(index, counts, sent, roots, left_roots, left_stats, right_stats):
     owners, slots, strip, tile = sent.shape
     lanes = left_stats.shape[1]
     dp = tile // lanes
@@ -515,15 +515,14 @@
             dma((2,)),
         ],
         compiler_params=pltpu.CompilerParams(
-            collective_id=0, has_side_effects=True, vmem_limit_bytes=40 * 1024 * 1024
+            collective_id=index, has_side_effects=True, vmem_limit_bytes=40 * 1024 * 1024
         ),
         cost_estimate=pl.CostEstimate(
             flops=8 * slots * lanes * tile * tile,
             bytes_accessed=slots * (12 * tile * tile + 20 * lanes * tile),
             transcendentals=0,
         ),
-        name="exchange",
-    )(sent, roots, left_roots, left_stats, right_stats)
+    )(sent, roots, left_roots, left_stats, right_stats)[:3]
 
 
 def inner(partial_grads, owner_map, left_stats, right_stats, left_roots, right_roots):
@@ -552,10 +551,20 @@
     )
     taken = jnp.take(shares, which, axis=0)
     sent = jnp.where(keep, taken, jnp.zeros((), taken.dtype))
-    counts = (slots, slots)
+    held = jnp.sum(filled.astype(jnp.int32), axis=1).reshape(owners // 2, 2)
+    most = jnp.max(held, axis=0)
+    levels = [k for k in range(slots // 2, slots - 2) if 2 * k + 2 >= slots]
+    plans = [(slots, slots)]
+    for k in levels:
+        plans += [(slots, k), (k, slots)]
+    fewest = jnp.min(most)
+    level = jnp.sum(jnp.array([fewest > k for k in levels]).astype(jnp.int32))
+    plan = 1 + 2 * level + (most[0] < most[1]).astype(jnp.int32)
+    plan = jnp.where(level == len(levels), 0, plan)
     shape = (slots, owners, strip, tile)
-    returned, new_left, new_right, _ = exchange(
-        counts,
+    returned, new_left, new_right = lax.switch(
+        plan,
+        [functools.partial(exchange, index, counts) for index, counts in enumerate(plans)],
         sent.reshape(owners, slots, strip, tile),
         right_roots[0].reshape(shape),
         left_roots[0],

time: 621 us -> 531 us (0.86)
  Pallas kernels: 433 us -> 346 us
  waiting for transfers between devices: 122 us -> 112 us
    pallas_call x1, Pallas kernels: 433 us -> 346 us  [exchange(): pl.pallas_call(functools.partial(exchange_kernel, counts), in_specs=[pl.B...]
    reduce_scatter x1, waiting for transfers between devices: 121 us -> 112 us  [inner(): lax.psum_scatter(partial_grads[0], 'dp', scatter_dimension=1, tiled=True)]
    unnamed x6 -> x10, local copies, waits for them, and re-layouts: 26.9 us -> 24.2 us
  transfers between devices with their start and end apart: 1 -> 1, of which waited for: 1 -> 1; matrix products, arithmetic and copies ran while one was open for 1% -> 2% of each run, Pallas kernels for 0% -> 0%
where the time goes in v1:
time: 531 us; the launch traced here: 530 us
  Pallas kernels  346 us (65%)
  waiting for transfers between devices  112 us (21%)
  local copies, waits for them, and re-layouts  39.6 us (7%)
  between operations  19.3 us (4%)
  other arithmetic  12.9 us (2%)
    pallas_call x1, Pallas kernels, exchange(): pl.pallas_call(functools.partial(exchange_kernel, counts), in_specs=[pl.B...  346 us
    reduce_scatter x1, waiting for transfers between devices, inner(): lax.psum_scatter(partial_grads[0], 'dp', scatter_dimension=1, tiled=True)  112 us
    unnamed x10, local copies, waits for them, and re-layouts  24.2 us
  transfers between devices with their start and end apart: 1, of which 1 were waited for; matrix products, arithmetic and copies ran while one was open for 2% of the time, Pallas kernels for 0%

profile of v1, /device:TPU:1, one launch (start us, length us, event | category | flops | bytes accessed | tf_op | source)
XLA Modules:
  0.0 530.3 jit_solution(18370372226480427162)
XLA Ops:
  7.2 0.7 reduce-scatter.2.cloned.1.call-update
  7.9 0.2 convert_reduce_fusion
  8.1 0.3 fusion
  8.6 0.3 and_reduce_fusion
  8.9 0.1 copy.9
  9.2 0.6 reduce_min.9
  12.4 0.6 fusion.17
  14.2 0.7 fusion.15
  16.3 1.2 gather_fusion.2
  17.5 1.2 gather_fusion.3
  19.2 0.6 compare_and_fusion.2
  19.8 0.6 pad_clamp_fusion
  20.3 0.7 broadcast_compare_fusion.1
  21.1 0.7 iota_compare_fusion.1
  21.8 0.1 iota_compare_fusion
  22.0 111.7 %reduce-scatter.2.cloned.1.call-done = bf16[48,32,1024]{2,1,0:T(8,128)(2,1)} async-done(((bf16[48,128,1024]{2,1,0:T(8,128)(2,1)}), bf16[48,32,1024]{2,1,0:T(8,128)(2,1)}) %reduce-scatter.2.cloned.1.call-update) | async-done | bytes 3145744 | tf_op jit(solution)/shard_map/reduce_scatter | solution.py:544
  133.6 7.9 %gather_fusion = bf16[96,32,1024]{2,1,0:T(8,128)(2,1)} fusion(bf16[48,32,1024]{2,1,0:T(8,128)(2,1)} %reduce-scatter.2.cloned.1.call-done, s32[1024]{0:T(1024)S(1)} %pad_clamp_fusion.1), kind=kCustom, calls=%fused_computation.2 | custom fusion | bytes 12583296 | tf_op jit(solution)/shard_map/jit(_take)/gather | solution.py:552
  141.5 5.1 and_select_fusion
  146.6 346.2 %conditional.1 = (bf16[8,12,32,1024]{3,2,1,0:T(8,128)(2,1)}, f32[12,256,1024]{2,1,0:T(8,128)}, f32[12,256,1024]{2,1,0:T(8,128)}) conditional(s32[]{:T(128)} %clamp.3, (bf16[8,12,32,1024]{3,2,1,0:T(8,128)(2,1)S(1)}, bf16[12,8,32,1024]{3,2,1,0:T(8,128)(2,1)}, bf16[12,256,1024]{2,1,0:T(8,128)(2,1)}, ...), branch_computations={%region_8.10_spmd, %region_9.11_spmd, %region_10.12_spmd, %region_... | conditional | flops 25769803776 | bytes 213909536 | solution.py:565
  146.9 345.7 %branch_4_fun.1 = (bf16[8,12,32,1024]{3,2,1,0:T(8,128)(2,1)}, f32[12,256,1024]{2,1,0:T(8,128)}, f32[12,256,1024]{2,1,0:T(8,128)}, bf16[24,4,8,32,1024]{4,3,2,1,0:T(8,128)(2,1)}) custom-call(bf16[8,12,32,1024]{3,2,1,0:T(8,128)(2,1)S(1)} %get-tuple-element.123.sent, bf16[12,8,32,1024]{3,2,1,0:T(8,128)(2,1)} %get-tuple-element.124.roots, ...), custom_call_target="tpu_custom_call" | custom-call | flops 25769803776 | bytes 213909504 | tf_op jit(solution)/shard_map/cond/branch_4_fun/pallas_call | solution.py:482
  492.8 3.7 gather_fusion.1
  496.6 2.7 and_select_fusion.1
  499.3 12.1 %copy.42 = f32[1,12,256,1024]{3,2,1,0:T(8,128)} copy(f32[1,12,256,1024]{3,2,1,0:T(8,128)} %bitcast.13) | data formatting | bytes 25165824
  511.4 12.1 %copy.43 = f32[1,12,256,1024]{3,2,1,0:T(8,128)} copy(f32[1,12,256,1024]{3,2,1,0:T(8,128)} %bitcast.14) | data formatting | bytes 25165824
  (32 shorter events, 0.9 us)
Async XLA Ops:
  7.2 126.5 %reduce-scatter.2.cloned.1.call-start = ((), (), s32[]{:S(2)}) async-start(), calls=%async_computation.1 | async-start | bytes 15728640 | tf_op jit(solution)/shard_map/reduce_scatter | solution.py:544
  7.2 0.7 copy-start.3
  492.8 3.7 copy-start
  492.8 3.7 copy-start.1
  492.8 3.7 copy-start.2
Sparse Core Ops, SparseCore 0:
  11.1 122.5 reduce-scatter.1

commit v2 on v0

--- a/solution.py
+++ b/solution.py
@@ -192,22 +192,248 @@
 MESH = pl.DeviceIdType.MESH
 
 
-def owner_slots(owner_map, owners, slots):
+def index_kernel(levels, owner_map, tile_of, place, held, plan):
     tiles = owner_map.shape[0]
-    ids = jnp.arange(tiles, dtype=jnp.int32)
-    same = (owner_map[:, None] == owner_map[None, :]) & (ids[None, :] < ids[:, None])
-    slot = jnp.sum(same.astype(jnp.int32), axis=1)
-    picks = (slot[None, None, :] == jnp.arange(slots, dtype=jnp.int32)[None, :, None]) & (
-        owner_map[None, None, :] == jnp.arange(owners, dtype=jnp.int32)[:, None, None]
-    )
-    tile_of = jnp.sum(jnp.where(picks, ids[None, None, :], 0), axis=2)
-    return slot, tile_of, jnp.any(picks, axis=2)
+    owners = held.shape[0]
+    slots = tile_of.shape[0] // owners
+
+    def each(count, act):
+        lax.fori_loop(0, count, lambda i, c: (act(i), c)[1], 0)
+
+    def clear(q):
+        tile_of[q] = tiles
+
+    def empty(o):
+        held[o] = 0
+
+    def take(t):
+        owner = owner_map[t]
+        slot = held[owner]
+        held[owner] = slot + 1
+        place[t] = owner * slots + slot
+        tile_of[owner * slots + slot] = t
+
+    each(owners * slots, clear)
+    each(owners, empty)
+    each(tiles, take)
+    most = [0, 0]
+    for o in range(owners):
+        most[o % 2] = jnp.maximum(most[o % 2], held[o])
+    fewest = jnp.minimum(most[0], most[1])
+    level = sum((fewest > k).astype(jnp.int32) for k in levels)
+    choice = 1 + 2 * level + (most[0] < most[1]).astype(jnp.int32)
+    plan[0] = jnp.where(level == len(levels), 0, choice)
+
+
+def indices(owner_map, owners, slots, levels):
+    tiles = owner_map.shape[0]
+    scalars = pl.BlockSpec(memory_space=pltpu.SMEM)
+    return pl.pallas_call(
+        functools.partial(index_kernel, levels),
+        in_specs=[scalars],
+        out_specs=[scalars] * 4,
+        out_shape=[
+            jax.ShapeDtypeStruct((size,), jnp.int32) for size in (owners * slots, tiles, owners, 1)
+        ],
+        name="indices",
+    )(owner_map)
+
+
+def reduce_kernel(
+    tile_of, rows, cols, partial, sent, mine_v, got_v, pass_v, last_v, shares_v,
+    load_sem, send_sem, recv_sem, pass_send, pass_recv,
+):
+    pairs, _, batch, _, strip, tile = mine_v.shape
+    owners, slots = sent.shape[:2]
+    own = lax.axis_index("owner")
+    me = lax.axis_index("dp")
+    x, y = me % 2, me // 2
+    across = me + 1 - 2 * x
+    along = me + 2 - 4 * y
+    peers = (across, along)
+    barrier = pltpu.get_barrier_semaphore()
+    for peer in peers:
+        pl.semaphore_signal(barrier, inc=1, device_id={"dp": peer}, device_id_type=MESH)
+
+    def each(count, act):
+        lax.fori_loop(0, count, lambda i, c: (act(i), c)[1], 0)
+
+    def blocks(p, way):
+        return pl.ds((2 * p + way) * batch, batch)
+
+    def load(p, way):
+        part = partial.at[blocks(p, 0), :, x] if way == 0 else partial.at[blocks(p, 1), y]
+        return pltpu.make_async_copy(part, mine_v.at[p, way], load_sem.at[p, way])
+
+    def give(p, way):
+        part = partial.at[blocks(p, 0), :, 1 - x] if way == 0 else partial.at[blocks(p, 1), 1 - y]
+        return pltpu.make_async_remote_copy(
+            src_ref=part,
+            dst_ref=got_v.at[p, way],
+            send_sem=send_sem.at[p, way],
+            recv_sem=recv_sem.at[p, way],
+            device_id={"dp": peers[way]},
+            device_id_type=MESH,
+        )
+
+    def hand(p, way):
+        return pltpu.make_async_remote_copy(
+            src_ref=pass_v.at[p, way],
+            dst_ref=last_v.at[p, way],
+            send_sem=pass_send.at[p, way],
+            recv_sem=pass_recv.at[p, way],
+            device_id={"dp": peers[1 - way]},
+            device_id_type=MESH,
+        )
+
+    def begin(p):
+        for way in (0, 1):
+            load(p, way).start()
+
+    def offer(p):
+        for way in (0, 1):
+            give(p, way).start()
+
+    def middle(p):
+        for way in (0, 1):
+            here = y if way == 0 else x
+            load(p, way).wait()
+            give(p, way).wait_recv()
+
+            def add(b):
+                total = mine_v[p, way, b, 1 - here].astype(jnp.float32)
+                total = total + got_v[p, way, b, 1 - here].astype(jnp.float32)
+                pass_v[p, way, b] = total.astype(jnp.bfloat16)
+
+            each(batch, add)
+            hand(p, way).start()
+
+    def finish(p):
+        for way in (0, 1):
+            here = y if way == 0 else x
+            hand(p, way).wait_recv()
+
+            def add(b):
+                t = (2 * p + way) * batch + b
+                total = mine_v[p, way, b, here].astype(jnp.float32)
+                total = total + got_v[p, way, b, here].astype(jnp.float32)
+                total = total + last_v[p, way, b].astype(jnp.float32)
+                first = own * (tile // owners) + me * strip
+                row = first + lax.broadcasted_iota(jnp.int32, total.shape, 0)
+                col = lax.broadcasted_iota(jnp.int32, total.shape, 1)
+                keep = (row < rows[t]) & (col < cols[t])
+                shares_v[t] = jnp.where(keep, total, 0.0).astype(jnp.bfloat16)
+
+            each(batch, add)
+
+    each(pairs, begin)
+    pl.semaphore_wait(barrier, 2)
+    each(pairs, offer)
+    shares_v[2 * pairs * batch] = jnp.zeros((strip, tile), jnp.bfloat16)
+    each(pairs, middle)
+    each(pairs, finish)
+
+    def fill(s):
+        for o in range(owners):
+            sent[o, s] = shares_v[tile_of[o * slots + s]]
+
+    each(slots, fill)
+
+    def ends(p):
+        for way in (0, 1):
+            give(p, way).wait_send()
+            hand(p, way).wait_send()
+
+    each(pairs, ends)
+
+
+def reduce(tile_of, rows, cols, partial, owners, slots):
+    tiles, _, _, strip, tile = partial.shape
+    batch = 4
+    pairs = tiles // (2 * batch)
+    scalars = pl.BlockSpec(memory_space=pltpu.SMEM)
+    bf16 = jnp.bfloat16
+    dma = pltpu.SemaphoreType.DMA
+    return pl.pallas_call(
+        reduce_kernel,
+        in_specs=[scalars] * 3 + [pl.BlockSpec(memory_space=pl.ANY)],
+        out_specs=pl.BlockSpec(memory_space=pltpu.VMEM),
+        out_shape=jax.ShapeDtypeStruct((owners, slots, strip, tile), bf16),
+        scratch_shapes=[
+            pltpu.VMEM((pairs, 2, batch, 2, strip, tile), bf16),
+            pltpu.VMEM((pairs, 2, batch, 2, strip, tile), bf16),
+            pltpu.VMEM((pairs, 2, batch, strip, tile), bf16),
+            pltpu.VMEM((pairs, 2, batch, strip, tile), bf16),
+            pltpu.VMEM((tiles + 1, strip, tile), bf16),
+        ]
+        + [dma((pairs, 2))] * 5,
+        compiler_params=pltpu.CompilerParams(
+            collective_id=0, has_side_effects=True, vmem_limit_bytes=48 * 1024 * 1024
+        ),
+        name="reduce",
+    )(tile_of, rows, cols, partial)
+
+
+def finish_kernel(place, rows, cols, held, *refs):
+    batch = len(refs) - 7
+    parts = refs[:batch]
+    left_gram, right_gram, left_stats, right_stats, direction, new_left, new_right = refs[batch:]
+    strip = direction.shape[1]
+    lanes = left_stats.shape[1]
+    own = lax.axis_index("owner")
+    step = pl.program_id(0)
+    filled = step < held[own]
+    for gram, stats, new in (
+        (left_gram, left_stats, new_left),
+        (right_gram, right_stats, new_right),
+    ):
+        term = jnp.where(filled, gram[0].astype(jnp.float32), 0.0)
+        new[0] = stat_decay * stats[0] + (1.0 - stat_decay) * term
+    first = lax.axis_index("dp") * lanes + own * strip
+    for b in range(batch):
+        t = step * batch + b
+        value = parts[b][0]
+        row = first + lax.broadcasted_iota(jnp.int32, value.shape, 0)
+        col = lax.broadcasted_iota(jnp.int32, value.shape, 1)
+        keep = (row < rows[t]) & (col < cols[t])
+        direction[b] = jnp.where(keep, value.astype(jnp.float32), 0.0).astype(jnp.bfloat16)
+
+
+def finish(place, rows, cols, held, flat, left_gram, right_gram, left_stats, right_stats):
+    slots, lanes, tile = left_stats.shape
+    tiles = place.shape[0]
+    strip = flat.shape[1]
+    batch = tiles // slots
+    part = lambda b: pl.BlockSpec(
+        (1, strip, tile), lambda s, place, *rest: (place[s * batch + b], 0, 0)
+    )
+    block = pl.BlockSpec((1, lanes, tile), lambda s, *rest: (s, 0, 0))
+    return pl.pallas_call(
+        finish_kernel,
+        grid_spec=pltpu.PrefetchScalarGridSpec(
+            num_scalar_prefetch=4,
+            grid=(slots,),
+            in_specs=[part(b) for b in range(batch)] + [block] * 4,
+            out_specs=[
+                pl.BlockSpec((batch, strip, tile), lambda s, *rest: (s, 0, 0)),
+                block,
+                block,
+            ],
+        ),
+        out_shape=[
+            jax.ShapeDtypeStruct((tiles, strip, tile), jnp.bfloat16),
+            jax.ShapeDtypeStruct(left_stats.shape, jnp.float32),
+            jax.ShapeDtypeStruct(left_stats.shape, jnp.float32),
+        ],
+        compiler_params=pltpu.CompilerParams(vmem_limit_bytes=60 * 1024 * 1024),
+        name="finish",
+    )(place, rows, cols, held, *([flat] * batch), left_gram, right_gram, left_stats, right_stats)
 
 
 def exchange_kernel(
-    counts, sent, roots, left_roots, left_stats, right_stats,
-    returned, new_left, new_right, wide,
-    g_v, r_v, l_v, ls_v, rs_v, part_v, mine_v, out_v, nl_v, nr_v,
+    counts, sent, roots, left_roots,
+    returned, left_gram, right_gram, wide,
+    g_v, r_v, l_v, part_v, mine_v, out_v, nl_v, nr_v,
     own_sem, to_send, to_recv, wide_send, wide_recv, back_send, back_recv, back_own,
     g_sem, r_sem, in_sem, nl_sem, nr_sem,
 ):
@@ -285,8 +511,6 @@
                 pltpu.make_async_copy(wide.at[s, panel], r_v.at[panel], r_sem.at[1 + index])
             )
         made.append(pltpu.make_async_copy(left_roots.at[s], l_v, in_sem.at[0]))
-        made.append(pltpu.make_async_copy(left_stats.at[s], ls_v, in_sem.at[1]))
-        made.append(pltpu.make_async_copy(right_stats.at[s], rs_v, in_sem.at[2]))
         return made
 
     def grads(s):
@@ -308,16 +532,16 @@
     def back_home(s, side):
         return pltpu.make_async_copy(out_v.at[side, own], returned.at[own, s], back_own.at[side])
 
-    def stats_out(s, side):
+    def grams_out(s, side):
         return (
-            pltpu.make_async_copy(nl_v.at[side], new_left.at[s], nl_sem.at[side]),
-            pltpu.make_async_copy(nr_v.at[side], new_right.at[s], nr_sem.at[side]),
+            pltpu.make_async_copy(nl_v.at[side], left_gram.at[s], nl_sem.at[side]),
+            pltpu.make_async_copy(nr_v.at[side], right_gram.at[s], nr_sem.at[side]),
         )
 
     def settle(s, side):
         sized(returned.at[0, pl.ds(0, owners - 1)], back_send.at[side]).wait()
         back_home(s, side).wait()
-        for copy in stats_out(s, side):
+        for copy in grams_out(s, side):
             copy.wait()
 
     width = lanes
@@ -363,14 +587,14 @@
 
         def third(c):
             right = dot(mine_v[...], column(c), ((1,), (0,)))
-            nr_v[side, :, cols(c)] = stat_decay * rs_v[:, cols(c)] + (1.0 - stat_decay) * right
+            nr_v[side, :, cols(c)] = right.astype(jnp.bfloat16)
             rows = g_v[pl.ds(me * pieces, pieces)].reshape(lanes, tile)
             block = g_v[pl.ds(c * pieces, pieces)].reshape(lanes, tile)
             left = dot(rows, block, ((1,), (1,)))
-            nl_v[side, :, cols(c)] = stat_decay * ls_v[:, cols(c)] + (1.0 - stat_decay) * left
+            nl_v[side, :, cols(c)] = left.astype(jnp.bfloat16)
 
         each(0, tile // width, third)
-        for copy in stats_out(s, side):
+        for copy in grams_out(s, side):
             copy.start()
 
         @pl.when(s + 1 < many)
@@ -428,25 +652,6 @@
     settle(many - 2, many % 2)
     settle(many - 1, (many + 1) % 2)
 
-    if min(counts) < slots:
-        def fade(s):
-            moved = [
-                pltpu.make_async_copy(left_stats.at[s], ls_v, in_sem.at[1]),
-                pltpu.make_async_copy(right_stats.at[s], rs_v, in_sem.at[2]),
-            ]
-            for copy in moved:
-                copy.start()
-            for copy in moved:
-                copy.wait()
-            nl_v[0] = stat_decay * ls_v[...]
-            nr_v[0] = stat_decay * rs_v[...]
-            for copy in stats_out(s, 0):
-                copy.start()
-            for copy in stats_out(s, 0):
-                copy.wait()
-
-        each(many, slots, fade)
-
     def sends(item):
         place = place_of(item)
         panel = wide.at[place, me]
@@ -472,34 +677,32 @@
         each(0, counts[p], ends)
 
 
-def exchange(counts, sent, roots, left_roots, left_stats, right_stats):
+def exchange(index, counts, sent, roots, left_roots):
     owners, slots, strip, tile = sent.shape
-    lanes = left_stats.shape[1]
+    lanes = left_roots.shape[1]
     dp = tile // lanes
     anywhere = pl.BlockSpec(memory_space=pl.ANY)
-    bf16, f32 = jnp.bfloat16, jnp.float32
+    bf16 = jnp.bfloat16
     dma = pltpu.SemaphoreType.DMA
     return pl.pallas_call(
         functools.partial(exchange_kernel, counts),
-        in_specs=[pl.BlockSpec(memory_space=pltpu.VMEM)] + [anywhere] * 4,
+        in_specs=[pl.BlockSpec(memory_space=pltpu.VMEM)] + [anywhere] * 2,
         out_specs=[anywhere] * 4,
         out_shape=[
             jax.ShapeDtypeStruct((owners, slots, strip, tile), bf16),
-            jax.ShapeDtypeStruct(left_stats.shape, f32),
-            jax.ShapeDtypeStruct(right_stats.shape, f32),
+            jax.ShapeDtypeStruct(left_roots.shape, bf16),
+            jax.ShapeDtypeStruct(left_roots.shape, bf16),
             jax.ShapeDtypeStruct((2 * slots, dp, owners, strip, tile), bf16),
         ],
         scratch_shapes=[
             pltpu.VMEM((owners, dp, strip, tile), bf16),
             pltpu.VMEM((dp, owners, strip, tile), bf16),
             pltpu.VMEM((lanes, tile), bf16),
-            pltpu.VMEM((lanes, tile), f32),
-            pltpu.VMEM((lanes, tile), f32),
             pltpu.VMEM((lanes, tile), bf16),
             pltpu.VMEM((lanes, tile), bf16),
             pltpu.VMEM((2, owners, strip, tile), bf16),
-            pltpu.VMEM((2, lanes, tile), f32),
-            pltpu.VMEM((2, lanes, tile), f32),
+            pltpu.VMEM((2, lanes, tile), bf16),
+            pltpu.VMEM((2, lanes, tile), bf16),
             dma((slots,)),
             dma((len(counts), slots)),
             dma((slots,)),
@@ -510,65 +713,58 @@
             dma((2,)),
             dma((dp,)),
             dma((dp,)),
-            dma((3,)),
+            dma((1,)),
             dma((2,)),
             dma((2,)),
         ],
         compiler_params=pltpu.CompilerParams(
-            collective_id=0, has_side_effects=True, vmem_limit_bytes=40 * 1024 * 1024
+            collective_id=1 + index, has_side_effects=True, vmem_limit_bytes=56 * 1024 * 1024
         ),
         cost_estimate=pl.CostEstimate(
             flops=8 * slots * lanes * tile * tile,
             bytes_accessed=slots * (12 * tile * tile + 20 * lanes * tile),
             transcendentals=0,
         ),
-        name="exchange",
-    )(sent, roots, left_roots, left_stats, right_stats)
+    )(sent, roots, left_roots)[:3]
 
 
 def inner(partial_grads, owner_map, left_stats, right_stats, left_roots, right_roots):
     dp = lax.axis_size("dp")
     owners = lax.axis_size("owner")
     slots, lanes, tile = left_stats.shape[1:]
-    if dp != 4 or owners % 2 or slots < 2:
+    tiles = owner_map.shape[0]
+    if dp != 4 or owners % 2 or slots < 6 or tiles % slots or tiles % 8:
         return general(
             partial_grads, owner_map, left_stats, right_stats, left_roots, right_roots
         )
-    owner_here = lax.axis_index("owner")
-    dp_here = lax.axis_index("dp")
-    tiles = owner_map.shape[0]
     strip = lanes // owners
     rows, cols = extents(tiles)
-    slot, tile_of, filled = owner_slots(owner_map, owners, slots)
-    line = jnp.arange(strip, dtype=jnp.int32)
-    wide_line = jnp.arange(tile, dtype=jnp.int32)
-    shares = lax.psum_scatter(partial_grads[0], "dp", scatter_dimension=1, tiled=True)
-    first = owner_here * (tile // owners) + dp_here * strip
-    which = tile_of.reshape(-1)
-    rows_of = jnp.where(filled.reshape(-1), jnp.take(rows, which), 0)
-    cols_of = jnp.take(cols, which)
-    keep = ((first + line)[None, :, None] < rows_of[:, None, None]) & (
-        wide_line[None, None, :] < cols_of[:, None, None]
-    )
-    taken = jnp.take(shares, which, axis=0)
-    sent = jnp.where(keep, taken, jnp.zeros((), taken.dtype))
-    counts = (slots, slots)
-    shape = (slots, owners, strip, tile)
-    returned, new_left, new_right, _ = exchange(
-        counts,
-        sent.reshape(owners, slots, strip, tile),
-        right_roots[0].reshape(shape),
+    levels = [k for k in range(slots // 2, slots - 2) if 2 * k + 2 >= slots]
+    plans = [(slots, slots)]
+    for k in levels:
+        plans += [(slots, k), (k, slots)]
+    tile_of, place, held, plan = indices(owner_map, owners, slots, levels)
+    sent = reduce(
+        tile_of, rows, cols, partial_grads[0].reshape(tiles, 2, 2, strip, tile), owners, slots
+    )
+    returned, left_gram, right_gram = lax.switch(
+        plan[0],
+        [functools.partial(exchange, index, counts) for index, counts in enumerate(plans)],
+        sent,
+        right_roots[0].reshape(slots, owners, strip, tile),
         left_roots[0],
+    )
+    direction, new_left, new_right = finish(
+        place,
+        rows,
+        cols,
+        held,
+        returned.reshape(owners * slots, strip, tile),
+        left_gram,
+        right_gram,
         left_stats[0],
         right_stats[0],
     )
-    first = dp_here * lanes + owner_here * strip
-    inside = ((first + line)[None, :, None] < rows[:, None, None]) & (
-        wide_line[None, None, :] < cols[:, None, None]
-    )
-    flat = returned.reshape(owners * slots, strip, tile)
-    direction = jnp.take(flat, owner_map * slots + slot, axis=0)
-    direction = jnp.where(inside, direction, jnp.zeros((), direction.dtype))
     return (direction, new_left[None], new_right[None])
 
 

time: 621 us -> 488 us (0.79)
  waiting for transfers between devices: 122 us -> 0 us
  Pallas kernels: 433 us -> 485 us
  local copies, waits for them, and re-layouts: 41.4 us -> 0.66 us
  between operations: 14.2 us -> 1.52 us
  other arithmetic: 9.06 us -> 0.02 us
    pallas_call x0 -> x3, Pallas kernels: none -> 138 us  [the longest x1 109 us: reduce(): pl.pallas_call(reduce_kernel, in_specs=[scalars] * 3 + [pl.BlockSpec(memo...]
    reduce_scatter x1 -> x0, waiting for transfers between devices: 121 us -> none  [inner(): lax.psum_scatter(partial_grads[0], 'dp', scatter_dimension=1, tiled=True)]
    pallas_call x1, Pallas kernels: 433 us -> 347 us  [exchange(): pl.pallas_call(functools.partial(exchange_kernel, counts), in_specs=[pl.B...]
    unnamed x6, local copies, waits for them, and re-layouts: 26.9 us -> 0.66 us
    gather x4 -> x0, local copies, waits for them, and re-layouts: 13.9 us -> none  [the longest x1 7.89 us: inner(): taken = jnp.take(shares, which, axis=0)]
    select_n x6 -> x0, other arithmetic: 7.83 us -> none  [the longest x1 5.11 us: inner(): sent = jnp.where(keep, taken, jnp.zeros((), taken.dtype))]
  transfers between devices with their start and end apart: 1 -> 0, of which waited for: 1 -> 0; matrix products, arithmetic and copies ran while one was open for 1% -> 0% of each run, Pallas kernels for 0% -> 0%
where the time goes in v2:
time: 488 us; the launch traced here: 487 us
  Pallas kernels  485 us (99%)
    pallas_call x1, Pallas kernels, exchange(): pl.pallas_call(functools.partial(exchange_kernel, counts), in_specs=[pl.B...  347 us
    pallas_call x1, Pallas kernels, reduce(): pl.pallas_call(reduce_kernel, in_specs=[scalars] * 3 + [pl.BlockSpec(memo...  109 us
    pallas_call x1, Pallas kernels, finish(): pl.pallas_call(finish_kernel, grid_spec=pltpu.PrefetchScalarGridSpec(num_...  25.9 us

profile of v2, /device:TPU:1, one launch (start us, length us, event | category | flops | bytes accessed | tf_op | source)
XLA Modules:
  0.0 487.2 jit_solution(13185986313505442604)
XLA Ops:
  0.7 0.0 copy-start
  0.7 0.0 copy-start.1
  0.7 2.5 indices.1
  3.8 0.0 copy-start.2
  3.9 0.6 copy-done.2
  4.5 109.3 %reduce.1 = bf16[8,12,32,1024]{3,2,1,0:T(8,128)(2,1)} custom-call(s32[96]{0:T(128)S(1)} %copy-done.2, s32[48]{0:T(128)S(1)} %get-tuple-element.132.rows, s32[48]{0:T(128)S(1)} %get-tuple-element.131.cols, bf16[48,2,2,32,1024]{4,3,2,1,0:T(8,128)(2,1)} %bitcast.9), custom_call_target="tpu_custom_call" | custom-call | tf_op jit(solution)/shard_map/reduce/pallas_call | solution.py:357
  113.8 0.0 copy-done
  113.8 0.0 copy-done.1
  113.8 347.3 %conditional.1 = (bf16[8,12,32,1024]{3,2,1,0:T(8,128)(2,1)}, bf16[12,256,1024]{2,1,0:T(8,128)(2,1)}, bf16[12,256,1024]{2,1,0:T(8,128)(2,1)}) conditional(s32[]{:T(128)} %bitcast, (bf16[8,12,32,1024]{3,2,1,0:T(8,128)(2,1)}, bf16[12,8,32,1024]{3,2,1,0:T(8,128)(2,1)}, bf16[12,256,1024]{2,1,0:T(8,128)(2,1)}) %tuple.65, ...), branch_computations={%region_0.1_spmd, %region_1.2_spmd, %region_2.3_spmd, %region_3.4_... | conditional | flops 25769803776 | bytes 213909536 | solution.py:750
  113.8 346.8 %branch_4_fun.1 = (bf16[8,12,32,1024]{3,2,1,0:T(8,128)(2,1)}, bf16[12,256,1024]{2,1,0:T(8,128)(2,1)}, bf16[12,256,1024]{2,1,0:T(8,128)(2,1)}, bf16[24,4,8,32,1024]{4,3,2,1,0:T(8,128)(2,1)}) custom-call(bf16[8,12,32,1024]{3,2,1,0:T(8,128)(2,1)} %get-tuple-element.78.sent, bf16[12,8,32,1024]{3,2,1,0:T(8,128)(2,1)} %get-tuple-element.79.roots, ...), custom_call_target="tpu_custom_call" | custom-call | flops 25769803776 | bytes 213909504 | tf_op jit(solution)/shard_map/cond/branch_4_fun/pallas_call | solution.py:687
  461.1 25.9 %finish.1 = (bf16[48,32,1024]{2,1,0:T(8,128)(2,1)}, f32[12,256,1024]{2,1,0:T(8,128)}, f32[12,256,1024]{2,1,0:T(8,128)}) custom-call(s32[48]{0:T(128)} %get-tuple-element.121.place, s32[48]{0:T(128)} %copy-done.1, s32[48]{0:T(128)} %copy-done, s32[8]{0:T(128)} %get-tuple-element.122.held, bf16[96,32,1024]{2,1,0:T(8,128)(2,1)} %bitcast.4.refs_0_.refs_1_.refs_2_.refs_3_, ...), custom_call_target="tpu_custom_call" | custom-call | tf_op jit(solution)/shard_map/finish/pallas_call | solution.py:411
  (1 shorter events, 0.0 us)
Async XLA Ops:
  0.7 113.1 %copy-start = (s32[48]{0:T(128)}, s32[48]{0:T(128)S(1)}, u32[]{:S(2)}) copy-start(s32[48]{0:T(128)S(1)} %get-tuple-element.131.cols) | copy-start | bytes 580
  0.7 113.1 %copy-start.1 = (s32[48]{0:T(128)}, s32[48]{0:T(128)S(1)}, u32[]{:S(2)}) copy-start(s32[48]{0:T(128)S(1)} %get-tuple-element.132.rows) | copy-start | bytes 580
  3.8 0.7 copy-start.2

commit v3 on v2

--- a/solution.py
+++ b/solution.py
@@ -374,68 +374,89 @@
     )(tile_of, rows, cols, partial)
 
 
-def finish_kernel(place, rows, cols, held, *refs):
-    batch = len(refs) - 7
-    parts = refs[:batch]
-    left_gram, right_gram, left_stats, right_stats, direction, new_left, new_right = refs[batch:]
-    strip = direction.shape[1]
-    lanes = left_stats.shape[1]
-    own = lax.axis_index("owner")
-    step = pl.program_id(0)
-    filled = step < held[own]
-    for gram, stats, new in (
-        (left_gram, left_stats, new_left),
-        (right_gram, right_stats, new_right),
-    ):
-        term = jnp.where(filled, gram[0].astype(jnp.float32), 0.0)
-        new[0] = stat_decay * stats[0] + (1.0 - stat_decay) * term
-    first = lax.axis_index("dp") * lanes + own * strip
-    for b in range(batch):
-        t = step * batch + b
-        value = parts[b][0]
+def finish_kernel(
+    place, rows, cols, flat, left, right, direction, new_left, new_right,
+    held_v, left_sem, right_sem, in_sem, out_sem,
+):
+    tiles, strip, _ = held_v.shape
+    slots, lanes = left.shape[:2]
+
+    def each(count, act):
+        lax.fori_loop(0, count, lambda i, c: (act(i), c)[1], 0)
+
+    def bring(t):
+        return pltpu.make_async_copy(flat.at[place[t]], held_v.at[t], in_sem.at[t])
+
+    def put(t):
+        return pltpu.make_async_copy(held_v.at[t], direction.at[t], out_sem.at[t])
+
+    def store(s):
+        return (
+            pltpu.make_async_copy(left.at[s], new_left.at[s], left_sem.at[s]),
+            pltpu.make_async_copy(right.at[s], new_right.at[s], right_sem.at[s]),
+        )
+
+    def start_all(s):
+        for copy in store(s):
+            copy.start()
+
+    def wait_all(s):
+        for copy in store(s):
+            copy.wait()
+
+    each(tiles, lambda t: bring(t).start())
+    each(slots, start_all)
+    first = lax.axis_index("dp") * lanes + lax.axis_index("owner") * strip
+
+    def mask(t):
+        bring(t).wait()
+        value = held_v[t].astype(jnp.float32)
         row = first + lax.broadcasted_iota(jnp.int32, value.shape, 0)
         col = lax.broadcasted_iota(jnp.int32, value.shape, 1)
         keep = (row < rows[t]) & (col < cols[t])
-        direction[b] = jnp.where(keep, value.astype(jnp.float32), 0.0).astype(jnp.bfloat16)
-
-
-def finish(place, rows, cols, held, flat, left_gram, right_gram, left_stats, right_stats):
-    slots, lanes, tile = left_stats.shape
+        held_v[t] = jnp.where(keep, value, 0.0).astype(jnp.bfloat16)
+        put(t).start()
+
+    each(tiles, mask)
+    each(tiles, lambda t: put(t).wait())
+    each(slots, wait_all)
+
+
+def finish(place, rows, cols, flat, left, right):
+    slots, _, tile = left.shape
     tiles = place.shape[0]
     strip = flat.shape[1]
-    batch = tiles // slots
-    part = lambda b: pl.BlockSpec(
-        (1, strip, tile), lambda s, place, *rest: (place[s * batch + b], 0, 0)
-    )
-    block = pl.BlockSpec((1, lanes, tile), lambda s, *rest: (s, 0, 0))
+    scalars = pl.BlockSpec(memory_space=pltpu.SMEM)
+    anywhere = pl.BlockSpec(memory_space=pltpu.HBM)
+    near = pl.BlockSpec(memory_space=pltpu.VMEM)
+    dma = pltpu.SemaphoreType.DMA
     return pl.pallas_call(
         finish_kernel,
-        grid_spec=pltpu.PrefetchScalarGridSpec(
-            num_scalar_prefetch=4,
-            grid=(slots,),
-            in_specs=[part(b) for b in range(batch)] + [block] * 4,
-            out_specs=[
-                pl.BlockSpec((batch, strip, tile), lambda s, *rest: (s, 0, 0)),
-                block,
-                block,
-            ],
-        ),
+        in_specs=[scalars] * 3 + [anywhere, near, near],
+        out_specs=[anywhere] * 3,
         out_shape=[
             jax.ShapeDtypeStruct((tiles, strip, tile), jnp.bfloat16),
-            jax.ShapeDtypeStruct(left_stats.shape, jnp.float32),
-            jax.ShapeDtypeStruct(left_stats.shape, jnp.float32),
+            jax.ShapeDtypeStruct(left.shape, jnp.float32),
+            jax.ShapeDtypeStruct(left.shape, jnp.float32),
         ],
-        compiler_params=pltpu.CompilerParams(vmem_limit_bytes=60 * 1024 * 1024),
+        scratch_shapes=[
+            pltpu.VMEM((tiles, strip, tile), jnp.bfloat16),
+            dma((slots,)),
+            dma((slots,)),
+            dma((tiles,)),
+            dma((tiles,)),
+        ],
+        compiler_params=pltpu.CompilerParams(vmem_limit_bytes=8 * 1024 * 1024),
         name="finish",
-    )(place, rows, cols, held, *([flat] * batch), left_gram, right_gram, left_stats, right_stats)
+    )(place, rows, cols, flat, left, right)
 
 
 def exchange_kernel(
-    counts, sent, roots, left_roots,
-    returned, left_gram, right_gram, wide,
-    g_v, r_v, l_v, part_v, mine_v, out_v, nl_v, nr_v,
+    counts, sent, roots, left_roots, left_stats, right_stats,
+    returned, new_left, new_right, wide,
+    g_v, r_v, l_v, part_v, mine_v, out_v,
     own_sem, to_send, to_recv, wide_send, wide_recv, back_send, back_recv, back_own,
-    g_sem, r_sem, in_sem, nl_sem, nr_sem,
+    g_sem, r_sem, in_sem, left_sem, right_sem,
 ):
     owners, slots, strip, tile = sent.shape
     lanes = left_roots.shape[1]
@@ -462,8 +483,18 @@
     def each(low, high, act):
         lax.fori_loop(low, high, lambda i, c: (act(i), c)[1], 0)
 
+    lead = min(4, min(counts))
+
+    def is_root(item):
+        late = item - 2 * lead
+        return (item < lead) | ((late >= 0) & (late % 2 == 1))
+
+    def slot_of(item):
+        late = lead + jnp.maximum(item - 2 * lead, 0) // 2
+        return jnp.where(item < lead, item, jnp.where(item < 2 * lead, item - lead, late))
+
     def place_of(item):
-        return jnp.where(item < many, item, slots + item - many)
+        return jnp.where(is_root(item), 0, slots) + slot_of(item)
 
     def own_copy(s):
         return pltpu.make_async_copy(
@@ -504,14 +535,22 @@
     def sized(ref, sem):
         return pltpu.make_async_copy(ref, ref, sem)
 
-    def loads(s):
+    def root_loads(s):
         made = [pltpu.make_async_copy(roots.at[s], r_v.at[me], r_sem.at[0])]
         for index, panel in enumerate((across, along, far)):
             made.append(
                 pltpu.make_async_copy(wide.at[s, panel], r_v.at[panel], r_sem.at[1 + index])
             )
-        made.append(pltpu.make_async_copy(left_roots.at[s], l_v, in_sem.at[0]))
         return made
+
+    def left_load(s):
+        return pltpu.make_async_copy(left_roots.at[s], l_v, in_sem.at[0])
+
+    def stats_in(s):
+        return (
+            pltpu.make_async_copy(left_stats.at[s], new_left.at[s], left_sem.at[s]),
+            pltpu.make_async_copy(right_stats.at[s], new_right.at[s], right_sem.at[s]),
+        )
 
     def grads(s):
         return [
@@ -532,83 +571,96 @@
     def back_home(s, side):
         return pltpu.make_async_copy(out_v.at[side, own], returned.at[own, s], back_own.at[side])
 
-    def grams_out(s, side):
-        return (
-            pltpu.make_async_copy(nl_v.at[side], left_gram.at[s], nl_sem.at[side]),
-            pltpu.make_async_copy(nr_v.at[side], right_gram.at[s], nr_sem.at[side]),
-        )
-
-    def settle(s, side):
+    def settle(side):
         sized(returned.at[0, pl.ds(0, owners - 1)], back_send.at[side]).wait()
-        back_home(s, side).wait()
-        for copy in grams_out(s, side):
-            copy.wait()
+        back_home(0, side).wait()
 
     width = lanes
 
-    def compute(s):
+    def cols(c):
+        return pl.ds(pl.multiple_of(c * width, width), width)
+
+    def column(c):
+        return g_v[:, :, :, cols(c)].reshape(tile, width)
+
+    def direct_part(s):
         side = s % 2
-        for copy in grads(s):
-            copy.start()
-
-        @pl.when(s == 0)
-        def _():
-            for copy in loads(0):
-                copy.start()
 
         @pl.when(s >= 2)
         def _():
-            settle(s - 2, side)
-
-        for copy in grads(s) + loads(s):
+            settle(side)
+
+        for copy in root_loads(s):
             copy.wait()
 
-        def cols(c):
-            return pl.ds(pl.multiple_of(c * width, width), width)
-
-        def column(c):
-            return g_v[:, :, :, cols(c)].reshape(tile, width)
-
-        def first(c):
-            part = dot(l_v[...], column(c), ((1,), (0,)))
-            part_v[:, cols(c)] = part.astype(jnp.bfloat16)
-
-        def second(c):
+        def act(c):
             right = r_v[:, :, :, cols(c)].reshape(tile, width)
             product = dot(part_v[...], right, ((1,), (0,)))
             out_v[side, :, :, cols(c)] = product.astype(jnp.bfloat16).reshape(owners, strip, width)
 
-        each(0, tile // width, first)
-        each(0, tile // width, second)
+        each(0, tile // width, act)
         for peer in others:
             back(s, side, peer).start()
         back_home(s, side).start()
+
+    def grads_part(s):
+        for copy in grads(s):
+            copy.start()
+
+        @pl.when(s < lead)
+        def _():
+            for copy in root_loads(s):
+                copy.start()
+
+        left_load(s).wait()
+        for copy in grads(s):
+            copy.wait()
+
+        def act(c):
+            part = dot(l_v[...], column(c), ((1,), (0,)))
+            part_v[:, cols(c)] = part.astype(jnp.bfloat16)
+
+        each(0, tile // width, act)
+
+        @pl.when(s + 1 < many)
+        def _():
+            left_load(s + 1).start()
+
+        @pl.when(s < lead)
+        def _():
+            direct_part(s)
+
+        for copy in stats_in(s):
+            copy.wait()
         mine_v[...] = column(me).T
 
-        def third(c):
+        def update(c):
             right = dot(mine_v[...], column(c), ((1,), (0,)))
-            nr_v[side, :, cols(c)] = right.astype(jnp.bfloat16)
+            old = new_right[s, :, cols(c)]
+            new_right[s, :, cols(c)] = stat_decay * old + (1.0 - stat_decay) * right
             rows = g_v[pl.ds(me * pieces, pieces)].reshape(lanes, tile)
             block = g_v[pl.ds(c * pieces, pieces)].reshape(lanes, tile)
             left = dot(rows, block, ((1,), (1,)))
-            nl_v[side, :, cols(c)] = left.astype(jnp.bfloat16)
-
-        each(0, tile // width, third)
-        for copy in grams_out(s, side):
+            old = new_left[s, :, cols(c)]
+            new_left[s, :, cols(c)] = stat_decay * old + (1.0 - stat_decay) * left
+
+        each(0, tile // width, update)
+
+    def begin(s):
+        for copy in stats_in(s):
             copy.start()
 
-        @pl.when(s + 1 < many)
+    each(0, slots, begin)
+    left_load(0).start()
+    each(0, many, lambda s: own_copy(s).start())
+
+    def turn(i):
+        slot = slot_of(i)
+
+        @pl.when((i < 2 * many) & is_root(i))
         def _():
-            for copy in loads(s + 1):
-                copy.start()
-
-    each(0, many, lambda s: own_copy(s).start())
-
-    def turn(i):
-        @pl.when(i < many)
-        def _():
-            direct(roots.at[i], i, 0, across).start()
-            direct(roots.at[i], i, 1, along).start()
+            direct(roots.at[slot], slot, 0, across).start()
+            direct(roots.at[slot], slot, 1, along).start()
 
         @pl.when(i < slots)
         def _():
@@ -621,13 +673,12 @@
                         def _():
                             give(i, peer).start()
 
-        @pl.when((i >= many) & (i < 2 * many))
+        @pl.when((i < 2 * many) & jnp.logical_not(is_root(i)))
         def _():
-            s = i - many
-            own_copy(s).wait()
-            sized(wide.at[slots + s, me, pl.ds(0, owners - 1)], to_recv.at[s]).wait()
-            direct(wide.at[slots + s, me], slots + s, 0, across).start()
-            direct(wide.at[slots + s, me], slots + s, 1, along).start()
+            own_copy(slot).wait()
+            sized(wide.at[slots + slot, me, pl.ds(0, owners - 1)], to_recv.at[slot]).wait()
+            direct(wide.at[slots + slot, me], slots + slot, 0, across).start()
+            direct(wide.at[slots + slot, me], slots + slot, 1, along).start()
 
         @pl.when((i >= 1) & (i < 2 * many + 1))
         def _():
@@ -640,17 +691,33 @@
         @pl.when(i >= 2)
         def _():
             place = place_of(i - 2)
+            done = slot_of(i - 2)
             sized(wide.at[place, far, pl.ds(0, half)], wide_recv.at[place, 2]).wait()
             sized(wide.at[place, far, pl.ds(half, half)], wide_recv.at[place, 3]).wait()
 
-        @pl.when(i >= many + 2)
-        def _():
-            compute(i - 2 - many)
+            @pl.when(is_root(i - 2) & (done >= lead))
+            def _():
+                for copy in root_loads(done):
+                    copy.start()
+                direct_part(done)
+
+            @pl.when(jnp.logical_not(is_root(i - 2)))
+            def _():
+                grads_part(done)
 
     each(0, 2 * many + 2, turn)
 
-    settle(many - 2, many % 2)
-    settle(many - 1, (many + 1) % 2)
+    settle(many % 2)
+    settle((many + 1) % 2)
+
+    if min(counts) < slots:
+        def fade(s):
+            for copy in stats_in(s):
+                copy.wait()
+            new_left[s] = stat_decay * new_left[s]
+            new_right[s] = stat_decay * new_right[s]
+
+        each(many, slots, fade)
 
     def sends(item):
         place = place_of(item)
@@ -677,21 +744,22 @@
         each(0, counts[p], ends)
 
 
-def exchange(index, counts, sent, roots, left_roots):
+def exchange(index, counts, sent, roots, left_roots, left_stats, right_stats):
     owners, slots, strip, tile = sent.shape
     lanes = left_roots.shape[1]
     dp = tile // lanes
-    anywhere = pl.BlockSpec(memory_space=pl.ANY)
+    anywhere = pl.BlockSpec(memory_space=pltpu.HBM)
+    near = pl.BlockSpec(memory_space=pltpu.VMEM)
     bf16 = jnp.bfloat16
     dma = pltpu.SemaphoreType.DMA
     return pl.pallas_call(
         functools.partial(exchange_kernel, counts),
-        in_specs=[pl.BlockSpec(memory_space=pltpu.VMEM)] + [anywhere] * 2,
-        out_specs=[anywhere] * 4,
+        in_specs=[near] + [anywhere] * 4,
+        out_specs=[anywhere, near, near, anywhere],
         out_shape=[
             jax.ShapeDtypeStruct((owners, slots, strip, tile), bf16),
-            jax.ShapeDtypeStruct(left_roots.shape, bf16),
-            jax.ShapeDtypeStruct(left_roots.shape, bf16),
+            jax.ShapeDtypeStruct(left_stats.shape, jnp.float32),
+            jax.ShapeDtypeStruct(left_stats.shape, jnp.float32),
             jax.ShapeDtypeStruct((2 * slots, dp, owners, strip, tile), bf16),
         ],
         scratch_shapes=[
@@ -701,8 +769,6 @@
             pltpu.VMEM((lanes, tile), bf16),
             pltpu.VMEM((lanes, tile), bf16),
             pltpu.VMEM((2, owners, strip, tile), bf16),
-            pltpu.VMEM((2, lanes, tile), bf16),
-            pltpu.VMEM((2, lanes, tile), bf16),
             dma((slots,)),
             dma((len(counts), slots)),
             dma((slots,)),
@@ -714,18 +780,18 @@
             dma((dp,)),
             dma((dp,)),
             dma((1,)),
-            dma((2,)),
-            dma((2,)),
+            dma((slots,)),
+            dma((slots,)),
         ],
         compiler_params=pltpu.CompilerParams(
-            collective_id=1 + index, has_side_effects=True, vmem_limit_bytes=56 * 1024 * 1024
+            collective_id=1 + index, has_side_effects=True, vmem_limit_bytes=16 * 1024 * 1024
         ),
         cost_estimate=pl.CostEstimate(
             flops=8 * slots * lanes * tile * tile,
             bytes_accessed=slots * (12 * tile * tile + 20 * lanes * tile),
             transcendentals=0,
         ),
-    )(sent, roots, left_roots)[:3]
+    )(sent, roots, left_roots, left_stats, right_stats)[:3]
 
 
 def inner(partial_grads, owner_map, left_stats, right_stats, left_roots, right_roots):
@@ -743,25 +809,28 @@
     plans = [(slots, slots)]
     for k in levels:
         plans += [(slots, k), (k, slots)]
-    tile_of, place, held, plan = indices(owner_map, owners, slots, levels)
+    tile_of, place, _, plan = indices(owner_map, owners, slots, levels)
     sent = reduce(
         tile_of, rows, cols, partial_grads[0].reshape(tiles, 2, 2, strip, tile), owners, slots
     )
-    returned, left_gram, right_gram = lax.switch(
+
+    def branch(index, counts):
+        def run(place, rows, cols, *operands):
+            returned, left, right = exchange(index, counts, *operands)
+            flat = returned.reshape(owners * slots, strip, tile)
+            return finish(place, rows, cols, flat, left, right)
+
+        return run
+
+    direction, new_left, new_right = lax.switch(
         plan[0],
-        [functools.partial(exchange, index, counts) for index, counts in enumerate(plans)],
+        [branch(index, counts) for index, counts in enumerate(plans)],
+        place,
+        rows,
+        cols,
         sent,
         right_roots[0].reshape(slots, owners, strip, tile),
         left_roots[0],
-    )
-    direction, new_left, new_right = finish(
-        place,
-        rows,
-        cols,
-        held,
-        returned.reshape(owners * slots, strip, tile),
-        left_gram,
-        right_gram,
         left_stats[0],
         right_stats[0],
     )

time: 488 us -> 468 us (0.959)
  Pallas kernels: 485 us -> 464 us
    pallas_call x2, Pallas kernels: 373 us -> 355 us  [the longest x1 340 us: exchange(): pl.pallas_call(functools.partial(exchange_kernel, counts), in_specs=[near...]
where the time goes in v3:
time: 468 us; the launch traced here: 467 us
  Pallas kernels  464 us (99%)
    pallas_call x1, Pallas kernels, exchange(): pl.pallas_call(functools.partial(exchange_kernel, counts), in_specs=[near...  340 us
    pallas_call x1, Pallas kernels, reduce(): pl.pallas_call(reduce_kernel, in_specs=[scalars] * 3 + [pl.BlockSpec(memo...  107 us
    pallas_call x1, Pallas kernels, finish(): pl.pallas_call(finish_kernel, in_specs=[scalars] * 3 + [anywhere, near, n...  15.4 us

profile of v3, /device:TPU:1, one launch (start us, length us, event | category | flops | bytes accessed | tf_op | source)
XLA Modules:
  0.0 466.9 jit_solution(4213346666301588129)
XLA Ops:
  0.7 2.6 indices.1
  3.9 0.0 copy-start
  3.9 0.6 copy-done
  4.5 0.0 copy-start.1
  4.6 106.7 %reduce.1 = bf16[8,12,32,1024]{3,2,1,0:T(8,128)(2,1)S(1)} custom-call(s32[96]{0:T(128)S(1)} %copy-done, s32[48]{0:T(128)S(1)} %get-tuple-element.458.rows, s32[48]{0:T(128)S(1)} %get-tuple-element.457.cols, bf16[48,2,2,32,1024]{4,3,2,1,0:T(8,128)(2,1)} %bitcast.58), custom_call_target="tpu_custom_call" | custom-call | tf_op jit(solution)/shard_map/reduce/pallas_call | solution.py:357
  111.2 0.0 copy-done.1
  111.2 355.5 %conditional.1 = ((bf16[48,32,1024]{2,1,0:T(8,128)(2,1)}, f32[12,256,1024]{2,1,0:T(8,128)}, f32[12,256,1024]{2,1,0:T(8,128)})) conditional(s32[]{:T(128)} %bitcast, (bf16[1,12,256,1024]{3,2,1,0:T(8,128)(2,1)S(1)}, bf16[1,12,256,1024]{3,2,1,0:T(8,128)(2,1)}, f32[1,12,256,1024]{3,2,1,0:T(8,128)}, ...), branch_computations={%region_0.1_spmd.clone, %region_1.2_spmd.clone, %region_2.3_spmd.c... | conditional | flops 25769803776 | bytes 213909504 | solution.py:825
  111.4 339.6 %branch_4_fun.1 = (bf16[8,12,32,1024]{3,2,1,0:T(8,128)(2,1)S(1)}, f32[12,256,1024]{2,1,0:T(8,128)S(1)}, f32[12,256,1024]{2,1,0:T(8,128)S(1)}, bf16[24,4,8,32,1024]{4,3,2,1,0:T(8,128)(2,1)}) custom-call(bf16[8,12,32,1024]{3,2,1,0:T(8,128)(2,1)S(1)} %get-tuple-element.400.sent, bf16[12,8,32,1024]{3,2,1,0:T(8,128)(2,1)S(1)} %bitcast.83, ...), custom_call_target="tpu_custom_call" | custom-call | flops 25769803776 | bytes 213909504 | tf_op jit(solution)/shard_map/cond/branch_4_fun/pallas_call | solution.py:755
  451.1 15.4 %finish.13 = (bf16[48,32,1024]{2,1,0:T(8,128)(2,1)}, f32[12,256,1024]{2,1,0:T(8,128)}, f32[12,256,1024]{2,1,0:T(8,128)}) custom-call(s32[48]{0:T(128)S(1)} %get-tuple-element.397.place, s32[48]{0:T(128)S(1)} %get-tuple-element.398.rows, s32[48]{0:T(128)S(1)} %get-tuple-element.399.cols, bf16[96,32,1024]{2,1,0:T(8,128)(2,1)S(1)} %bitcast.53, ...), custom_call_target="tpu_custom_call" | custom-call | tf_op jit(solution)/shard_map/cond/branch_4_fun/finish/pallas_call | solution.py:433
  (1 shorter events, 0.0 us)
Async XLA Ops:
  3.9 0.7 copy-start
  4.5 106.7 %copy-start.1 = (bf16[1,12,256,1024]{3,2,1,0:T(8,128)(2,1)S(1)}, bf16[1,12,256,1024]{3,2,1,0:T(8,128)(2,1)}, u32[]{:S(2)}) copy-start(bf16[1,12,256,1024]{3,2,1,0:T(8,128)(2,1)} %param.20) | copy-start | bytes 18874372
